TPU v7x, 32 devices: a whole 2x2x4 slice. The times are simulated.
32 devices in a mesh: blk: 8 (over z, x), rows: 4 (over y, core).
Axes of the slice: x: 2, y: 2, z: 4, core: 2. Of those that a mesh axis runs over, the one named last changes fastest.
Arguments:
- centers: int32 [512, 1], P(('blk', 'rows')), may hold values from 0 to 127, as said below
- gates_used: int32 [512], P(('blk', 'rows')), may hold values from 12 to 40
- jacobian: bfloat16 [512, 3, 40, 256], P(('blk', 'rows')), may hold values from -0.3984375 to 0.3984375
- weights: bfloat16 [512, 40], P(('blk', 'rows')), may hold values from 0.099609375 to 1
Outputs:
- hessian_band: float32 [128, 3, 256, 256], P(('blk', 'rows'))
Inputs may be any that keep to these rules, and one draw needn't show every extreme that they name: `centers`: cell block c is owned by blk index c // 16. Among the soundings of one device at most 4 are centred on blocks of one owner, and some owner gets exactly 4 of them; the number a device sends to the owner k places further along blk (cyclically) is the same for all devices of one rows index. Among the soundings of all devices of one rows index at most 2 share a centre block, and some block has exactly 2.
All inputs are finite; a program needn't handle non-finite values.
Results may differ from a plain program's by a relative error of at most 0.0024.
Values may be sent and summed in bfloat16 or wider, within the bound.
No kernel may reach another device: no remote copies, remote signals or barrier semaphores. Data moves between devices by JAX's collectives and lax.ppermute only.
A program may use at most 128 MiB of HBM per device.

v0:
```python
import jax
import jax.numpy as jnp
from jax import lax
from jax.sharding import PartitionSpec as P

KB = 16


def with_halo(block, sides, width):
    for axis, dim in sides:
        count = lax.axis_size(axis)
        forward = [(i, i + 1) for i in range(count - 1)]
        backward = [(target, source) for source, target in forward]
        low = lax.ppermute(
            lax.slice_in_dim(block, block.shape[dim] - width, None, axis=dim), axis, forward
        )
        high = lax.ppermute(lax.slice_in_dim(block, 0, width, axis=dim), axis, backward)
        block = jnp.concatenate([low, block, high], axis=dim)
    return block


def rank_among(labels):
    positions = jnp.arange(labels.shape[0], dtype=jnp.int32)
    before = (labels[None, :] == labels[:, None]) & (positions[None, :] < positions[:, None])
    return jnp.sum(before.astype(jnp.int32), axis=1)


def band_terms(buckets, bucket_wts, base, total_blocks):
    block_num, slot_len, foot_len, gate_len, cell_len = buckets.shape
    grid_pos = (
        base
        + jnp.arange(block_num, dtype=jnp.int32)[:, None]
        + jnp.arange(foot_len, dtype=jnp.int32)[None, :]
        - 1
    )
    inside = ((grid_pos >= 0) & (grid_pos < total_blocks)).astype(jnp.float32)
    scaled = (
        buckets.astype(jnp.float32)
        * bucket_wts.astype(jnp.float32)[:, :, None, :, None]
        * inside[:, None, :, None, None]
    ).astype(jnp.bfloat16)
    masked = buckets * inside.astype(jnp.bfloat16)[:, None, :, None, None]
    accum = jnp.zeros((block_num + 2, foot_len, cell_len, cell_len), jnp.float32)
    for lead_pos in range(foot_len):
        left = scaled[:, :, lead_pos].reshape(block_num, slot_len * gate_len, cell_len)
        for offset in range(foot_len - lead_pos):
            right = masked[:, :, lead_pos + offset].reshape(
                block_num, slot_len * gate_len, cell_len
            )
            term = lax.dot_general(
                left, right, (((1,), (1,)), ((0,), (0,))), preferred_element_type=jnp.float32
            )
            accum = accum.at[lead_pos : lead_pos + block_num, offset].add(term)
    return accum


def edge_rows(accum):
    return jnp.stack([accum[0], accum[accum.shape[0] - 1]])


def attach(accum, padded):
    block_num = accum.shape[0] - 2
    core = accum[1 : block_num + 1]
    core = core.at[0].add(padded[0])
    return core.at[block_num - 1].add(padded[3])


def on_device(centers, gates_used, jacobian, weights):
    blk_count = lax.axis_size("blk")
    sound_count, foot_len, gate_len, cell_len = jacobian.shape
    capacity = max(2, 2 * sound_count // blk_count)
    bucket_cap = max(2, 2 * sound_count // KB)
    slot_count = blk_count * capacity
    total_blocks = blk_count * KB
    centre_ids = centers[:, 0]
    owner = centre_ids // KB
    within = centre_ids - owner * KB
    order_in = rank_among(owner)
    gate_live = jnp.arange(gate_len, dtype=jnp.int32)[None, :] < gates_used[:, None]
    weight_live = jnp.where(gate_live, weights, jnp.zeros_like(weights))
    target = owner * capacity + order_in
    select = (target[None, :] == jnp.arange(slot_count, dtype=jnp.int32)[:, None]).astype(
        jnp.bfloat16
    )
    packed = (
        jnp.dot(select, jacobian.reshape(sound_count, -1), preferred_element_type=jnp.float32)
        .astype(jnp.bfloat16)
        .reshape(slot_count, foot_len, gate_len, cell_len)
    )
    packed_wts = jnp.dot(select, weight_live, preferred_element_type=jnp.float32).astype(
        jnp.bfloat16
    )
    packed_ids = jnp.dot(
        select, (within + 1).astype(jnp.bfloat16)[:, None], preferred_element_type=jnp.float32
    ).astype(jnp.bfloat16)[:, 0]
    received, received_wts, received_ids = (
        lax.all_to_all(packed, "blk", split_axis=0, concat_axis=0, tiled=True),
        lax.all_to_all(packed_wts, "blk", split_axis=0, concat_axis=0, tiled=True),
        lax.all_to_all(packed_ids, "blk", split_axis=0, concat_axis=0, tiled=True),
    )
    arrived_ids = received_ids.astype(jnp.int32)
    arrived_rank = rank_among(arrived_ids)
    bucket_target = jnp.where(arrived_ids > 0, (arrived_ids - 1) * bucket_cap + arrived_rank, -1)
    bucket_count = KB * bucket_cap
    bucket_sel = (
        bucket_target[None, :] == jnp.arange(bucket_count, dtype=jnp.int32)[:, None]
    ).astype(jnp.bfloat16)
    buckets = (
        jnp.dot(bucket_sel, received.reshape(slot_count, -1), preferred_element_type=jnp.float32)
        .astype(jnp.bfloat16)
        .reshape(KB, bucket_cap, foot_len, gate_len, cell_len)
    )
    bucket_wts = (
        jnp.dot(bucket_sel, received_wts, preferred_element_type=jnp.float32)
        .astype(jnp.bfloat16)
        .reshape(KB, bucket_cap, gate_len)
    )
    mine_blk = lax.axis_index("blk")
    share = KB // lax.axis_size("rows")
    moved, moved_wts = (
        lax.all_to_all(buckets, "rows", split_axis=0, concat_axis=1, tiled=True),
        lax.all_to_all(bucket_wts, "rows", split_axis=0, concat_axis=1, tiled=True),
    )
    base = mine_blk * KB + lax.axis_index("rows") * share
    accum = band_terms(moved, moved_wts, base, total_blocks)
    padded = with_halo(edge_rows(accum), ((("blk", "rows"), 0),), 1)
    return attach(accum, padded)


def solution(mesh):
    placed = (
        P(("blk", "rows"), None),
        P(("blk", "rows")),
        P(("blk", "rows"), None, None, None),
        P(("blk", "rows"), None),
    )
    return jax.shard_map(
        on_device,
        mesh=mesh,
        in_specs=placed,
        out_specs=P(("blk", "rows"), None, None, None),
        check_vma=False,
    )
```

profile of v0, /device:TPU:3, one launch (start us, length us, event | category | flops | bytes accessed | tf_op | source)
XLA Modules:
  0.0 140.4 jit_solution(17639520557241093231)
XLA Ops:
  0.0 0.7 and_select_fusion.1
  0.7 0.7 fusion.55
  1.3 0.2 convert_reduce_fusion.1
  1.5 0.7 multiply_add_fusion
  2.2 0.8 fusion.9
  3.0 0.7 all_to_all.48
  3.6 5.8 %all-to-all-start = ((bf16[8,4,1]{1,2,0:T(2,128)(2,1)}), bf16[8,4,1]{1,2,0:T(2,128)(2,1)S(1)}, u32[]{:S(2)}, u32[]{:S(2)}) async-start(bf16[8,4,1]{1,2,0:T(2,128)(2,1)} %all_to_all.48), calls=%async_computation | async-start | bytes 8192 | tf_op jit(solution)/shard_map/all_to_all | solution.py:99
  9.4 1.5 %convolution_convert_fusion.3 = bf16[32,40]{1,0:T(8,128)(2,1)} fusion(s32[16]{0:T(128)S(1)} %multiply_add_fusion, bf16[16,40]{1,0:T(8,128)(2,1)} %param.23, s32[16]{0:T(128)} %param.21), kind=kOutput, calls=%fused_computation.21 | convolution fusion | flops 44032 | bytes 3968 | tf_op jit(solution)/shard_map/dot_general | solution.py:90
  10.9 1.4 copy.23
  12.3 1.2 all-to-all-done
  13.5 4.4 %all-to-all-start.3 = ((bf16[8,4,40]{2,1,0:T(4,128)(2,1)}), bf16[8,4,40]{2,1,0:T(4,128)(2,1)S(1)}, u32[]{:S(2)}, u32[]{:S(2)}) async-start(bf16[8,4,40]{2,1,0:T(4,128)(2,1)} %bitcast.7), calls=%async_computation.3 | async-start | bytes 16384 | tf_op jit(solution)/shard_map/all_to_all | solution.py:98
  17.9 0.6 convolution_convert_fusion.1
  18.6 1.7 %copy.24 = bf16[4,8,120,256]{3,2,1,0:T(8,128)(2,1)} copy(bf16[4,8,120,256]{3,1,2,0:T(8,128)(2,1)S(1)} %bitcast.109) | data formatting | bytes 3932160
  20.2 1.9 %all-to-all-done.3 = bf16[8,4,40]{2,1,0:T(4,128)(2,1)S(1)} async-done(((bf16[8,4,40]{2,1,0:T(4,128)(2,1)}), bf16[8,4,40]{2,1,0:T(4,128)(2,1)S(1)}, u32[]{:S(2)}, u32[]{:S(2)}) %all-to-all-start.3) | async-done | bytes 2592 | tf_op jit(solution)/shard_map/all_to_all | solution.py:98
  22.1 4.7 %all-to-all-start.1 = ((bf16[32,3,40,256]{3,2,1,0:T(8,128)(2,1)}), bf16[32,3,40,256]{3,2,1,0:T(8,128)(2,1)S(1)}, u32[]{:S(2)}, u32[]{:S(2)}) async-start(bf16[32,3,40,256]{3,2,1,0:T(8,128)(2,1)} %bitcast.108), calls=%async_computation.1 | async-start | bytes 3932160 | tf_op jit(solution)/shard_map/all_to_all | solution.py:97
  26.9 0.2 convert_reduce_fusion
  27.2 0.7 reshape.492
  27.9 43.5 %all-to-all-done.1 = bf16[32,3,40,256]{3,2,1,0:T(8,128)(2,1)S(1)} async-done(((bf16[32,3,40,256]{3,2,1,0:T(8,128)(2,1)}), bf16[32,3,40,256]{3,2,1,0:T(8,128)(2,1)S(1)}, u32[]{:S(2)}, u32[]{:S(2)}) %all-to-all-start.1) | async-done | bytes 1966112 | tf_op jit(solution)/shard_map/all_to_all | solution.py:97
  71.5 4.7 %all-to-all-start.4 = ((bf16[4,2,160]{2,1,0:T(2,128)(2,1)}), bf16[4,2,160]{2,1,0:T(2,128)(2,1)S(1)}, u32[]{:S(2)}, u32[]{:S(2)}) async-start(bf16[4,2,160]{2,1,0:T(2,128)(2,1)} %reshape.492), calls=%async_computation.4 | async-start | bytes 8192 | tf_op jit(solution)/shard_map/all_to_all | solution.py:122
  76.1 0.4 copy.25
  76.5 0.7 convolution_convert_fusion
  77.2 1.7 %copy.26 = bf16[4,8,120,256]{3,2,1,0:T(8,128)(2,1)} copy(bf16[4,8,120,256]{3,1,2,0:T(8,128)(2,1)S(1)} %bitcast.111) | data formatting | bytes 3932160
  78.9 0.4 all-to-all-done.4
  79.2 4.3 %all-to-all-start.2 = ((bf16[16,2,3,40,256]{4,3,2,1,0:T(8,128)(2,1)}), bf16[16,2,3,40,256]{4,3,2,1,0:T(8,128)(2,1)S(1)}, u32[]{:S(2)}, u32[]{:S(2)}) async-start(bf16[16,2,3,40,256]{4,3,2,1,0:T(8,128)(2,1)} %bitcast.42), calls=%async_computation.2 | async-start | bytes 3932160 | tf_op jit(solution)/shard_map/all_to_all | solution.py:121
  83.5 0.6 fusion.38
  84.1 0.6 fusion.37
  84.7 0.8 and_reduce_fusion
  85.6 21.2 %all-to-all-done.2 = bf16[16,2,3,40,256]{4,3,2,1,0:T(8,128)(2,1)S(1)} async-done(((bf16[16,2,3,40,256]{4,3,2,1,0:T(8,128)(2,1)}), bf16[16,2,3,40,256]{4,3,2,1,0:T(8,128)(2,1)S(1)}, u32[]{:S(2)}, u32[]{:S(2)}) %all-to-all-start.2) | async-done | bytes 1966112 | tf_op jit(solution)/shard_map/all_to_all | solution.py:121
  106.8 0.2 copy.19
  107.0 0.5 multiply_convert_fusion
  107.5 0.2 fusion.35
  107.7 0.2 broadcast_multiply_fusion
  107.9 0.2 fusion.36
  108.0 0.5 convolution_bitcast_fusion.5
  108.5 0.5 scatter-add.26
  109.0 1.7 %fusion.1 = f32[6,3,256,256]{3,2,0,1:T(8,128)S(1)} fusion(f32[6,3,256,256]{3,2,0,1:T(8,128)S(1)} %scatter-add.26, s32[]{:T(128)} %bitcast.16, s32[]{:T(128)} %bitcast.17, bf16[4,320,256]{2,1,0:T(8,128)(2,1)S(1)} %bitcast.101, bf16[4,320,256]{2,1,0:T(8,128)(2,1)S(1)} %bitcast.114, f32[4,1,256,256]{3,2,0,1:T(8,128)S(1)} %convolution_bitcast_fusion.5), kind=kOutput, calls=%fused_computation.12 | convolution fusion | flops 168034304 | bytes 3407880 | tf_op jit(solution)/shard_map/dot_general | solution.py:50
  110.7 2.4 %fusion.8 = f32[6,3,256,256]{3,2,0,1:T(8,128)S(1)} fusion(f32[6,3,256,256]{3,2,0,1:T(8,128)S(1)} %fusion.1, s32[]{:T(128)} %bitcast.20, s32[]{:T(128)} %bitcast.21, bf16[4,320,256]{2,1,0:T(8,128)(2,1)S(1)} %bitcast.102, bf16[4,320,256]{2,1,0:T(8,128)(2,1)S(1)} %bitcast.103, pred[]{:T(512)} %and_reduce_fusion), kind=kOutput, calls=%fused_computation.19 | convolution fusion | flops 168296448 | bytes 3407881 | tf_op jit(solution)/shard_map/dot_general | solution.py:50
  113.2 0.6 fusion.3
  113.8 0.6 fusion.5
  114.4 0.6 fusion.7
  115.1 0.2 fusion.34
  115.2 2.9 %collective-permute-start = (f32[1,3,256,256]{3,2,0,1:T(8,128)S(1)}, f32[1,3,256,256]{3,2,0,1:T(8,128)S(1)}, u32[]{:S(2)}, u32[]{:S(2)}) collective-permute-start(f32[1,3,256,256]{3,2,0,1:T(8,128)S(1)} %get-tuple-element.102), channel_id=1, source_target_pairs={{0,1},{1,2},{2,3},{3,4},{4,5},{5,6},{6,7},{7,8},{8,9},{9,10},{10,1... | collective-permute-start | bytes 2359304 | tf_op jit(solution)/shard_map/ppermute | solution.py:14
  118.1 1.9 %collective-permute-start.1 = (f32[1,3,256,256]{3,2,0,1:T(8,128)S(1)}, f32[1,3,256,256]{3,2,0,1:T(8,128)S(1)}, u32[]{:S(2)}, u32[]{:S(2)}) collective-permute-start(f32[1,3,256,256]{3,2,0,1:T(8,128)S(1)} %get-tuple-element.101), channel_id=1, source_target_pairs={{1,0},{2,1},{3,2},{4,3},{5,4},{6,5},{7,6},{8,7},{9,8},{10,9},{11,1... | collective-permute-start | bytes 2359304 | tf_op jit(solution)/shard_map/ppermute | solution.py:17
  120.1 0.2 slice.306
  120.3 15.2 %collective-permute-done = f32[1,3,256,256]{3,2,0,1:T(8,128)S(1)} collective-permute-done((f32[1,3,256,256]{3,2,0,1:T(8,128)S(1)}, f32[1,3,256,256]{3,2,0,1:T(8,128)S(1)}, u32[]{:S(2)}, u32[]{:S(2)}) %collective-permute-start) | collective-permute-done | bytes 786464 | tf_op jit(solution)/shard_map/ppermute | solution.py:14
  135.6 2.6 %collective-permute-done.1 = f32[1,3,256,256]{3,2,0,1:T(8,128)S(1)} collective-permute-done((f32[1,3,256,256]{3,2,0,1:T(8,128)S(1)}, f32[1,3,256,256]{3,2,0,1:T(8,128)S(1)}, u32[]{:S(2)}, u32[]{:S(2)}) %collective-permute-start.1) | collective-permute-done | bytes 786464 | tf_op jit(solution)/shard_map/ppermute | solution.py:17
  138.2 0.2 fusion.10
  138.3 2.1 %copy.22 = f32[4,3,256,256]{3,2,1,0:T(8,128)} copy(f32[4,3,256,256]{3,2,0,1:T(8,128)S(1)} %fusion.10) | data formatting | bytes 6291456 | tf_op jit(solution)/shard_map/scatter-add | solution.py:65
  (15 shorter events, 0.5 us)
Async XLA Ops:
  3.6 9.9 %all-to-all-start = ((bf16[8,4,1]{1,2,0:T(2,128)(2,1)}), bf16[8,4,1]{1,2,0:T(2,128)(2,1)S(1)}, u32[]{:S(2)}, u32[]{:S(2)}) async-start(bf16[8,4,1]{1,2,0:T(2,128)(2,1)} %all_to_all.48), calls=%async_computation | async-start | bytes 8192 | tf_op jit(solution)/shard_map/all_to_all | solution.py:99
  13.5 8.6 %all-to-all-start.3 = ((bf16[8,4,40]{2,1,0:T(4,128)(2,1)}), bf16[8,4,40]{2,1,0:T(4,128)(2,1)S(1)}, u32[]{:S(2)}, u32[]{:S(2)}) async-start(bf16[8,4,40]{2,1,0:T(4,128)(2,1)} %bitcast.7), calls=%async_computation.3 | async-start | bytes 16384 | tf_op jit(solution)/shard_map/all_to_all | solution.py:98
  22.1 49.3 %all-to-all-start.1 = ((bf16[32,3,40,256]{3,2,1,0:T(8,128)(2,1)}), bf16[32,3,40,256]{3,2,1,0:T(8,128)(2,1)S(1)}, u32[]{:S(2)}, u32[]{:S(2)}) async-start(bf16[32,3,40,256]{3,2,1,0:T(8,128)(2,1)} %bitcast.108), calls=%async_computation.1 | async-start | bytes 3932160 | tf_op jit(solution)/shard_map/all_to_all | solution.py:97
  71.5 7.8 %all-to-all-start.4 = ((bf16[4,2,160]{2,1,0:T(2,128)(2,1)}), bf16[4,2,160]{2,1,0:T(2,128)(2,1)S(1)}, u32[]{:S(2)}, u32[]{:S(2)}) async-start(bf16[4,2,160]{2,1,0:T(2,128)(2,1)} %reshape.492), calls=%async_computation.4 | async-start | bytes 8192 | tf_op jit(solution)/shard_map/all_to_all | solution.py:122
  77.2 7.5 %copy-start = (s32[4]{0:T(128)S(1)}, s32[4]{0:T(128)}, u32[]{:S(2)}) copy-start(s32[4]{0:T(128)} %constant.269.clone.1) | copy-start | bytes 52
  79.2 27.6 %all-to-all-start.2 = ((bf16[16,2,3,40,256]{4,3,2,1,0:T(8,128)(2,1)}), bf16[16,2,3,40,256]{4,3,2,1,0:T(8,128)(2,1)S(1)}, u32[]{:S(2)}, u32[]{:S(2)}) async-start(bf16[16,2,3,40,256]{4,3,2,1,0:T(8,128)(2,1)} %bitcast.42), calls=%async_computation.2 | async-start | bytes 3932160 | tf_op jit(solution)/shard_map/all_to_all | solution.py:121
  115.2 20.2 %collective-permute-start = (f32[1,3,256,256]{3,2,0,1:T(8,128)S(1)}, f32[1,3,256,256]{3,2,0,1:T(8,128)S(1)}, u32[]{:S(2)}, u32[]{:S(2)}) collective-permute-start(f32[1,3,256,256]{3,2,0,1:T(8,128)S(1)} %get-tuple-element.102), channel_id=1, source_target_pairs={{0,1},{1,2},{2,3},{3,4},{4,5},{5,6},{6,7},{7,8},{8,9},{9,10},{10,1... | collective-permute-start | bytes 2359304 | tf_op jit(solution)/shard_map/ppermute | solution.py:14
  118.1 20.0 %collective-permute-start.1 = (f32[1,3,256,256]{3,2,0,1:T(8,128)S(1)}, f32[1,3,256,256]{3,2,0,1:T(8,128)S(1)}, u32[]{:S(2)}, u32[]{:S(2)}) collective-permute-start(f32[1,3,256,256]{3,2,0,1:T(8,128)S(1)} %get-tuple-element.101), channel_id=1, source_target_pairs={{1,0},{2,1},{3,2},{4,3},{5,4},{6,5},{7,6},{8,7},{9,8},{10,9},{11,1... | collective-permute-start | bytes 2359304 | tf_op jit(solution)/shard_map/ppermute | solution.py:17
where the time goes:
time: 141 us; the launch traced here: 140 us
  waiting for transfers between devices  86 us (61%)
  starting transfers between devices  28.6 us (20%)
  local copies, waits for them, and re-layouts  11.3 us (8%)
  matrix products  10.2 us (7%)
  other arithmetic  4.17 us (3%)
    all_to_all x1, waiting for transfers between devices, on_device(): lax.all_to_all(packed, 'blk', split_axis=0, concat_axis=0, tiled=True)  43.5 us
    all_to_all x1, waiting for transfers between devices, on_device(): lax.all_to_all(buckets, 'rows', split_axis=0, concat_axis=1, tiled=True)  21.2 us
    ppermute x1, waiting for transfers between devices, with_halo(): lax.ppermute(lax.slice_in_dim(block, block.shape[dim] - width, None, axis...  15.2 us
    dot_general x6, matrix products, band_terms(): lax.dot_general(left, right, (((1,), (1,)), ((0,), (0,))), preferred_elem...  6.5 us
    unnamed x8, local copies, waits for them, and re-layouts  5.87 us
    all_to_all x1, starting transfers between devices, on_device(): lax.all_to_all(packed_ids, 'blk', split_axis=0, concat_axis=0, tiled=True)  5.78 us
    all_to_all x1, starting transfers between devices, on_device(): lax.all_to_all(packed, 'blk', split_axis=0, concat_axis=0, tiled=True)  4.71 us
    all_to_all x1, starting transfers between devices, on_device(): lax.all_to_all(bucket_wts, 'rows', split_axis=0, concat_axis=1, tiled=True)  4.67 us
  transfers between devices with their start and end apart: 7, of which 7 were waited for; matrix products, arithmetic and copies ran while one was open for 8% of the time, Pallas kernels for 0%

commit v1 on v0

--- a/solution.py
+++ b/solution.py
@@ -4,6 +4,22 @@
 from jax.sharding import PartitionSpec as P
 
 KB = 16
+
+
+def swapped_with_each(x, axis, split, join):
+    ways, here = (lax.axis_size(axis), lax.axis_index(axis))
+    width = x.shape[split] // ways
+    shape = list(x.shape)
+    shape[split] = width
+    height = shape[join]
+    shape[join] = height * ways
+    full = jnp.zeros(shape, x.dtype)
+    for mask in range(ways):
+        part = lax.dynamic_slice_in_dim(x, (here ^ mask) * width, width, axis=split)
+        if mask:
+            part = lax.ppermute(part, axis, [(d, d ^ mask) for d in range(ways)])
+        full = lax.dynamic_update_slice_in_dim(full, part, (here ^ mask) * height, axis=join)
+    return full
 
 
 def with_halo(block, sides, width):
@@ -118,7 +134,7 @@
     mine_blk = lax.axis_index("blk")
     share = KB // lax.axis_size("rows")
     moved, moved_wts = (
-        lax.all_to_all(buckets, "rows", split_axis=0, concat_axis=1, tiled=True),
+        swapped_with_each(buckets, "rows", 0, 1),
         lax.all_to_all(bucket_wts, "rows", split_axis=0, concat_axis=1, tiled=True),
     )
     base = mine_blk * KB + lax.axis_index("rows") * share

time: 141 us -> 135 us (0.957)
  waiting for transfers between devices: 86 us -> 83.3 us
  starting transfers between devices: 28.6 us -> 26.8 us
    all_to_all x1 -> x0, waiting for transfers between devices: 21.2 us -> none  [on_device(): lax.all_to_all(buckets, 'rows', split_axis=0, concat_axis=1, tiled=True)]
    ppermute x0 -> x3, waiting for transfers between devices: none -> 20.8 us  [swapped_with_each(): part = lax.ppermute(part, axis, [(d, d ^ mask) for d in range(ways)])]
    all_to_all x1 -> x0, starting transfers between devices: 4.27 us -> none  [on_device(): lax.all_to_all(buckets, 'rows', split_axis=0, concat_axis=1, tiled=True)]
    ppermute x0 -> x3, starting transfers between devices: none -> 2.51 us  [swapped_with_each(): part = lax.ppermute(part, axis, [(d, d ^ mask) for d in range(ways)])]
  transfers between devices with their start and end apart: 7 -> 9, of which waited for: 7 -> 8; matrix products, arithmetic and copies ran while one was open for 8% -> 8% of each run, Pallas kernels for 0% -> 0%
where the time goes in v1:
time: 135 us
  waiting for transfers between devices  83.3 us (62%)
  starting transfers between devices  26.8 us (20%)
  local copies, waits for them, and re-layouts  10.3 us (8%)
  matrix products  10.1 us (7%)
  other arithmetic  4.13 us (3%)
    all_to_all x1, waiting for transfers between devices, on_device(): lax.all_to_all(packed, 'blk', split_axis=0, concat_axis=0, tiled=True)  42.2 us
    ppermute x3, waiting for transfers between devices, swapped_with_each(): part = lax.ppermute(part, axis, [(d, d ^ mask) for d in range(ways)])  20.8 us
    ppermute x1, waiting for transfers between devices, with_halo(): lax.ppermute(lax.slice_in_dim(block, block.shape[dim] - width, None, axis...  15.2 us
    dot_general x6, matrix products, band_terms(): lax.dot_general(left, right, (((1,), (1,)), ((0,), (0,))), preferred_elem...  6.48 us
    all_to_all x1, starting transfers between devices, on_device(): lax.all_to_all(packed_ids, 'blk', split_axis=0, concat_axis=0, tiled=True)  5.78 us
    all_to_all x1, starting transfers between devices, on_device(): lax.all_to_all(packed, 'blk', split_axis=0, concat_axis=0, tiled=True)  4.71 us
    all_to_all x1, starting transfers between devices, on_device(): lax.all_to_all(bucket_wts, 'rows', split_axis=0, concat_axis=1, tiled=True)  4.67 us
    unnamed x8, local copies, waits for them, and re-layouts  4.6 us
  transfers between devices with their start and end apart: 9, of which 8 were waited for; matrix products, arithmetic and copies ran while one was open for 8% of the time, Pallas kernels for 0%

profile of v1, /device:TPU:3, one launch (start us, length us, event | category | flops | bytes accessed | tf_op | source)
XLA Modules:
  0.0 134.9 jit_solution(18354022045185620302)
XLA Ops:
  0.0 0.7 and_select_fusion.1
  0.7 0.7 fusion.55
  1.3 0.2 convert_reduce_fusion.1
  1.5 0.7 multiply_add_fusion
  2.2 0.8 fusion.9
  3.0 0.7 all_to_all.31
  3.6 5.8 %all-to-all-start = ((bf16[8,4,1]{1,2,0:T(2,128)(2,1)}), bf16[8,4,1]{1,2,0:T(2,128)(2,1)S(1)}, u32[]{:S(2)}, u32[]{:S(2)}) async-start(bf16[8,4,1]{1,2,0:T(2,128)(2,1)} %all_to_all.31), calls=%async_computation | async-start | bytes 8192 | tf_op jit(solution)/shard_map/all_to_all | solution.py:115
  9.4 1.5 %convolution_convert_fusion.3 = bf16[32,40]{1,0:T(8,128)(2,1)} fusion(s32[16]{0:T(128)S(1)} %multiply_add_fusion, bf16[16,40]{1,0:T(8,128)(2,1)} %param.23, s32[16]{0:T(128)} %param.21), kind=kOutput, calls=%fused_computation.21 | convolution fusion | flops 44032 | bytes 3968 | tf_op jit(solution)/shard_map/dot_general | solution.py:106
  10.9 1.4 %copy.38 = bf16[2,8,120,256]{3,1,2,0:T(8,128)(2,1)S(1)} copy(bf16[2,8,120,256]{3,2,1,0:T(8,128)(2,1)} %bitcast.113) | data formatting | bytes 1966080
  12.3 1.2 all-to-all-done
  13.5 4.4 %all-to-all-start.2 = ((bf16[8,4,40]{2,1,0:T(4,128)(2,1)}), bf16[8,4,40]{2,1,0:T(4,128)(2,1)S(1)}, u32[]{:S(2)}, u32[]{:S(2)}) async-start(bf16[8,4,40]{2,1,0:T(4,128)(2,1)} %bitcast.4), calls=%async_computation.2 | async-start | bytes 16384 | tf_op jit(solution)/shard_map/all_to_all | solution.py:114
  17.9 0.6 convolution_convert_fusion.1
  18.6 1.7 %copy.39 = bf16[4,8,120,256]{3,2,1,0:T(8,128)(2,1)} copy(bf16[4,8,120,256]{3,1,2,0:T(8,128)(2,1)S(1)} %bitcast.103) | data formatting | bytes 3932160
  20.2 1.9 %all-to-all-done.2 = bf16[8,4,40]{2,1,0:T(4,128)(2,1)S(1)} async-done(((bf16[8,4,40]{2,1,0:T(4,128)(2,1)}), bf16[8,4,40]{2,1,0:T(4,128)(2,1)S(1)}, u32[]{:S(2)}, u32[]{:S(2)}) %all-to-all-start.2) | async-done | bytes 2592 | tf_op jit(solution)/shard_map/all_to_all | solution.py:114
  22.1 4.7 %all-to-all-start.1 = ((bf16[32,3,40,256]{3,2,1,0:T(8,128)(2,1)}), bf16[32,3,40,256]{3,2,1,0:T(8,128)(2,1)S(1)}, u32[]{:S(2)}, u32[]{:S(2)}) async-start(bf16[32,3,40,256]{3,2,1,0:T(8,128)(2,1)} %bitcast.102), calls=%async_computation.1 | async-start | bytes 3932160 | tf_op jit(solution)/shard_map/all_to_all | solution.py:113
  26.8 0.6 fusion.37
  27.4 0.7 and_reduce_fusion
  28.3 0.2 convert_reduce_fusion
  28.6 0.7 reshape.492
  29.3 42.2 %all-to-all-done.1 = bf16[32,3,40,256]{3,2,1,0:T(8,128)(2,1)S(1)} async-done(((bf16[32,3,40,256]{3,2,1,0:T(8,128)(2,1)}), bf16[32,3,40,256]{3,2,1,0:T(8,128)(2,1)S(1)}, u32[]{:S(2)}, u32[]{:S(2)}) %all-to-all-start.1) | async-done | bytes 1966112 | tf_op jit(solution)/shard_map/all_to_all | solution.py:113
  71.5 4.7 %all-to-all-start.3 = ((bf16[4,2,160]{2,1,0:T(2,128)(2,1)}), bf16[4,2,160]{2,1,0:T(2,128)(2,1)S(1)}, u32[]{:S(2)}, u32[]{:S(2)}) async-start(bf16[4,2,160]{2,1,0:T(2,128)(2,1)} %reshape.492), calls=%async_computation.3 | async-start | bytes 8192 | tf_op jit(solution)/shard_map/all_to_all | solution.py:138
  76.1 0.4 copy.40
  76.5 0.7 convolution_convert_fusion
  77.2 0.4 copy.41
  77.8 0.6 fusion.38
  78.4 0.8 all-to-all-done.3
  79.3 1.0 collective-permute-start.1
  80.3 1.4 %collective-permute-start.2 = (bf16[4,2,3,40,256]{4,3,2,1,0:T(8,128)(2,1)S(1)}, bf16[4,2,3,40,256]{4,3,2,1,0:T(8,128)(2,1)S(1)}, u32[]{:S(2)}, u32[]{:S(2)}) collective-permute-start(bf16[4,2,3,40,256]{4,3,2,1,0:T(8,128)(2,1)S(1)} %get-tuple-element.109), channel_id=1, source_target_pairs={{0,3},{1,2},{2,1},{3,0},{4,7},{5,6},{6,5},{7,4},{8,11},{9,10},{10,... | collective-permute-start | bytes 1474568 | tf_op jit(solution)/shard_map/ppermute | solution.py:20
  81.7 0.2 broadcast_in_dim.5
  82.0 9.4 %collective-permute-done.1 = bf16[4,2,3,40,256]{4,3,2,1,0:T(8,128)(2,1)S(1)} collective-permute-done((bf16[4,2,3,40,256]{4,3,2,1,0:T(8,128)(2,1)S(1)}, bf16[4,2,3,40,256]{4,3,2,1,0:T(8,128)(2,1)S(1)}, u32[]{:S(2)}, u32[]{:S(2)}) %collective-permute-start.1) | collective-permute-done | bytes 491552 | tf_op jit(solution)/shard_map/ppermute | solution.py:20
  91.5 11.3 %collective-permute-done.2 = bf16[4,2,3,40,256]{4,3,2,1,0:T(8,128)(2,1)S(1)} collective-permute-done((bf16[4,2,3,40,256]{4,3,2,1,0:T(8,128)(2,1)S(1)}, bf16[4,2,3,40,256]{4,3,2,1,0:T(8,128)(2,1)S(1)}, u32[]{:S(2)}, u32[]{:S(2)}) %collective-permute-start.2) | collective-permute-done | bytes 491552 | tf_op jit(solution)/shard_map/ppermute | solution.py:20
  102.9 0.5 multiply_convert_fusion
  103.6 0.2 broadcast_multiply_fusion
  104.0 0.5 convolution_bitcast_fusion.5
  104.5 0.5 scatter-add.26
  105.0 1.7 %fusion.1 = f32[6,3,256,256]{3,2,0,1:T(8,128)S(1)} fusion(f32[6,3,256,256]{3,2,0,1:T(8,128)S(1)} %scatter-add.26, s32[]{:T(128)} %bitcast.13, s32[]{:T(128)} %bitcast.14, bf16[4,320,256]{2,1,0:T(8,128)(2,1)S(1)} %bitcast.95, bf16[4,320,256]{2,1,0:T(8,128)(2,1)S(1)} %bitcast.108, f32[4,1,256,256]{3,2,0,1:T(8,128)S(1)} %convolution_bitcast_fusion.5), kind=kOutput, calls=%fused_computation.12 | convolution fusion | flops 168034304 | bytes 3407880 | tf_op jit(solution)/shard_map/dot_general | solution.py:66
  106.7 2.4 %fusion.8 = f32[6,3,256,256]{3,2,0,1:T(8,128)S(1)} fusion(f32[6,3,256,256]{3,2,0,1:T(8,128)S(1)} %fusion.1, s32[]{:T(128)} %bitcast.17, s32[]{:T(128)} %bitcast.18, bf16[4,320,256]{2,1,0:T(8,128)(2,1)S(1)} %bitcast.96, bf16[4,320,256]{2,1,0:T(8,128)(2,1)S(1)} %bitcast.97, pred[]{:T(512)} %and_reduce_fusion), kind=kOutput, calls=%fused_computation.19 | convolution fusion | flops 168296448 | bytes 3407881 | tf_op jit(solution)/shard_map/dot_general | solution.py:66
  109.1 0.6 fusion.3
  109.7 0.6 fusion.5
  110.4 0.6 fusion.7
  111.0 0.2 fusion.34
  111.2 2.8 %collective-permute-start.3 = (f32[1,3,256,256]{3,2,0,1:T(8,128)S(1)}, f32[1,3,256,256]{3,2,0,1:T(8,128)S(1)}, u32[]{:S(2)}, u32[]{:S(2)}) collective-permute-start(f32[1,3,256,256]{3,2,0,1:T(8,128)S(1)} %get-tuple-element.102), channel_id=1, source_target_pairs={{0,1},{1,2},{2,3},{3,4},{4,5},{5,6},{6,7},{7,8},{8,9},{9,10},{10,1... | collective-permute-start | bytes 2359304 | tf_op jit(solution)/shard_map/ppermute | solution.py:30
  114.0 1.9 %collective-permute-start.4 = (f32[1,3,256,256]{3,2,0,1:T(8,128)S(1)}, f32[1,3,256,256]{3,2,0,1:T(8,128)S(1)}, u32[]{:S(2)}, u32[]{:S(2)}) collective-permute-start(f32[1,3,256,256]{3,2,0,1:T(8,128)S(1)} %get-tuple-element.101), channel_id=1, source_target_pairs={{1,0},{2,1},{3,2},{4,3},{5,4},{6,5},{7,6},{8,7},{9,8},{10,9},{11,1... | collective-permute-start | bytes 2359304 | tf_op jit(solution)/shard_map/ppermute | solution.py:33
  115.9 0.2 slice.306
  116.1 15.2 %collective-permute-done.3 = f32[1,3,256,256]{3,2,0,1:T(8,128)S(1)} collective-permute-done((f32[1,3,256,256]{3,2,0,1:T(8,128)S(1)}, f32[1,3,256,256]{3,2,0,1:T(8,128)S(1)}, u32[]{:S(2)}, u32[]{:S(2)}) %collective-permute-start.3) | collective-permute-done | bytes 786464 | tf_op jit(solution)/shard_map/ppermute | solution.py:30
  131.4 1.2 collective-permute-done.4
  132.6 0.2 fusion.10
  132.8 2.1 %copy.37 = f32[4,3,256,256]{3,2,1,0:T(8,128)} copy(f32[4,3,256,256]{3,2,0,1:T(8,128)S(1)} %fusion.10) | data formatting | bytes 6291456 | tf_op jit(solution)/shard_map/scatter-add | solution.py:81
  (24 shorter events, 1.2 us)
Async XLA Ops:
  3.6 9.9 %all-to-all-start = ((bf16[8,4,1]{1,2,0:T(2,128)(2,1)}), bf16[8,4,1]{1,2,0:T(2,128)(2,1)S(1)}, u32[]{:S(2)}, u32[]{:S(2)}) async-start(bf16[8,4,1]{1,2,0:T(2,128)(2,1)} %all_to_all.31), calls=%async_computation | async-start | bytes 8192 | tf_op jit(solution)/shard_map/all_to_all | solution.py:115
  13.5 8.6 %all-to-all-start.2 = ((bf16[8,4,40]{2,1,0:T(4,128)(2,1)}), bf16[8,4,40]{2,1,0:T(4,128)(2,1)S(1)}, u32[]{:S(2)}, u32[]{:S(2)}) async-start(bf16[8,4,40]{2,1,0:T(4,128)(2,1)} %bitcast.4), calls=%async_computation.2 | async-start | bytes 16384 | tf_op jit(solution)/shard_map/all_to_all | solution.py:114
  18.6 8.9 %copy-start = (s32[4]{0:T(128)S(1)}, s32[4]{0:T(128)}, u32[]{:S(2)}) copy-start(s32[4]{0:T(128)} %constant.276.clone.1) | copy-start | bytes 52
  22.1 49.3 %all-to-all-start.1 = ((bf16[32,3,40,256]{3,2,1,0:T(8,128)(2,1)}), bf16[32,3,40,256]{3,2,1,0:T(8,128)(2,1)S(1)}, u32[]{:S(2)}, u32[]{:S(2)}) async-start(bf16[32,3,40,256]{3,2,1,0:T(8,128)(2,1)} %bitcast.102), calls=%async_computation.1 | async-start | bytes 3932160 | tf_op jit(solution)/shard_map/all_to_all | solution.py:113
  71.5 7.8 %all-to-all-start.3 = ((bf16[4,2,160]{2,1,0:T(2,128)(2,1)}), bf16[4,2,160]{2,1,0:T(2,128)(2,1)S(1)}, u32[]{:S(2)}, u32[]{:S(2)}) async-start(bf16[4,2,160]{2,1,0:T(2,128)(2,1)} %reshape.492), calls=%async_computation.3 | async-start | bytes 8192 | tf_op jit(solution)/shard_map/all_to_all | solution.py:138
  77.7 4.2 %collective-permute-start = (bf16[4,2,3,40,256]{4,3,2,1,0:T(8,128)(2,1)S(1)}, bf16[4,2,3,40,256]{4,3,2,1,0:T(8,128)(2,1)S(1)}, u32[]{:S(2)}, u32[]{:S(2)}) collective-permute-start(bf16[4,2,3,40,256]{4,3,2,1,0:T(8,128)(2,1)S(1)} %get-tuple-element.111), channel_id=1, source_target_pairs={{0,1},{1,0},{2,3},{3,2},{4,5},{5,4},{6,7},{7,6},{8,9},{9,8},{10,11... | collective-permute-start | bytes 1474568 | tf_op jit(solution)/shard_map/ppermute | solution.py:20
  79.3 12.1 %collective-permute-start.1 = (bf16[4,2,3,40,256]{4,3,2,1,0:T(8,128)(2,1)S(1)}, bf16[4,2,3,40,256]{4,3,2,1,0:T(8,128)(2,1)S(1)}, u32[]{:S(2)}, u32[]{:S(2)}) collective-permute-start(bf16[4,2,3,40,256]{4,3,2,1,0:T(8,128)(2,1)S(1)} %get-tuple-element.110), channel_id=1, source_target_pairs={{0,2},{1,3},{2,0},{3,1},{4,6},{5,7},{6,4},{7,5},{8,10},{9,11},{10,... | collective-permute-start | bytes 1474568 | tf_op jit(solution)/shard_map/ppermute | solution.py:20
  80.3 22.6 %collective-permute-start.2 = (bf16[4,2,3,40,256]{4,3,2,1,0:T(8,128)(2,1)S(1)}, bf16[4,2,3,40,256]{4,3,2,1,0:T(8,128)(2,1)S(1)}, u32[]{:S(2)}, u32[]{:S(2)}) collective-permute-start(bf16[4,2,3,40,256]{4,3,2,1,0:T(8,128)(2,1)S(1)} %get-tuple-element.109), channel_id=1, source_target_pairs={{0,3},{1,2},{2,1},{3,0},{4,7},{5,6},{6,5},{7,4},{8,11},{9,10},{10,... | collective-permute-start | bytes 1474568 | tf_op jit(solution)/shard_map/ppermute | solution.py:20
  111.2 20.2 %collective-permute-start.3 = (f32[1,3,256,256]{3,2,0,1:T(8,128)S(1)}, f32[1,3,256,256]{3,2,0,1:T(8,128)S(1)}, u32[]{:S(2)}, u32[]{:S(2)}) collective-permute-start(f32[1,3,256,256]{3,2,0,1:T(8,128)S(1)} %get-tuple-element.102), channel_id=1, source_target_pairs={{0,1},{1,2},{2,3},{3,4},{4,5},{5,6},{6,7},{7,8},{8,9},{9,10},{10,1... | collective-permute-start | bytes 2359304 | tf_op jit(solution)/shard_map/ppermute | solution.py:30
  114.0 18.6 %collective-permute-start.4 = (f32[1,3,256,256]{3,2,0,1:T(8,128)S(1)}, f32[1,3,256,256]{3,2,0,1:T(8,128)S(1)}, u32[]{:S(2)}, u32[]{:S(2)}) collective-permute-start(f32[1,3,256,256]{3,2,0,1:T(8,128)S(1)} %get-tuple-element.101), channel_id=1, source_target_pairs={{1,0},{2,1},{3,2},{4,3},{5,4},{6,5},{7,6},{8,7},{9,8},{10,9},{11,1... | collective-permute-start | bytes 2359304 | tf_op jit(solution)/shard_map/ppermute | solution.py:33
